TPU v7x, 256 devices: a whole 4x4x8 slice. The times are simulated.
256 devices in a mesh: pop: 64 (over z, y, core), tp: 4 (over x).
Axes of the slice: x: 4, y: 4, z: 8, core: 2. Of those that a mesh axis runs over, the one named last changes fastest.
Arguments:
- tokens: bfloat16 [65536, 5120], P('pop', 'tp'), may hold values from -6 to 6
- target: bfloat16 [65536, 5120], P('pop', 'tp'), may hold values from -6 to 6
- weight: bfloat16 [5120, 5120], P('pop', 'tp'), may hold values from -6 to 6
- factor_out: bfloat16 [256, 4, 5120], P('pop'), may hold values from -6 to 6
- factor_in: bfloat16 [256, 4, 5120], P('pop', None, 'tp'), may hold values from -6 to 6
Outputs:
- perturbed: bfloat16 [65536, 5120], P('pop', 'tp')
- new_weight: bfloat16 [5120, 5120], P('pop', 'tp')
All inputs are finite; a program needn't handle non-finite values.
Results may differ from a plain program's by a relative error of at most 0.012.
Values may be sent and summed in bfloat16 or wider, within the bound.
A program may use at most 128 MiB of HBM per device.

v0:
```python
import math
import jax
import jax.numpy as jnp
from jax import lax
from jax.sharding import PartitionSpec as P

noise_scale = 0.25
step_scale = 10.0


def sent_to_all(shard, axis):
    count = lax.axis_size(axis)
    return lax.all_to_all(
        jnp.broadcast_to(shard[None], (count, *shard.shape)), axis, 0, 0, tiled=True
    )


def taken_together(shard, axis):
    everything = sent_to_all(shard, axis)
    return jnp.sum(everything, axis=0)


def local(tokens, target, weight, factor_out, factor_in):
    tok_rows, shard_width = tokens.shape
    mem_local, rank, width_out = factor_out.shape
    tok_member = tok_rows // mem_local
    tp_count = lax.axis_size("tp")
    width_in = shard_width * tp_count
    out_cols = width_out // tp_count
    col_first = lax.axis_index("tp") * out_cols
    base_factor = 1.0 / math.sqrt(width_in)
    token_sets = tokens.reshape(mem_local, tok_member, shard_width)
    codes_part = jnp.einsum(
        "mkc,mrc->mkr", token_sets, factor_in, preferred_element_type=jnp.float32
    )
    codes_sum = taken_together(codes_part, "tp")
    partial_terms = (
        lax.dot_general(
            tokens,
            lax.all_gather(weight, "pop", axis=0, tiled=True),
            (((1,), (1,)), ((), ())),
            preferred_element_type=jnp.float32,
        )
        * base_factor
    )
    base_sum = lax.psum_scatter(
        partial_terms.astype(jnp.bfloat16), "tp", scatter_dimension=1, tiled=True
    ).astype(jnp.float32)
    outer_cols = lax.dynamic_slice_in_dim(factor_out, col_first, out_cols, 2).astype(jnp.float32)
    low_rank = jnp.einsum(
        "mkr,mrc->mkc", codes_sum, outer_cols, precision=lax.Precision.HIGHEST
    ) * (noise_scale / math.sqrt(rank * width_in))
    output_full = base_sum.reshape(mem_local, tok_member, out_cols) + low_rank
    wanted = target.reshape(mem_local, tok_member, out_cols).astype(jnp.float32)
    fitness_part = jnp.sum(output_full * wanted, axis=(1, 2)) / (tok_member * math.sqrt(width_out))
    fitness_grid = lax.all_gather(fitness_part[None, :], ("pop", "tp"), axis=0, tiled=True)
    fitness_all = jnp.sum(fitness_grid.reshape(-1, tp_count, mem_local), axis=1).reshape(-1)
    outer_rows = lax.all_to_all(factor_out, "pop", split_axis=2, concat_axis=0, tiled=True)
    inner_cols = lax.all_gather(factor_in, "pop", axis=0, tiled=True)
    centered = fitness_all - jnp.mean(fitness_all)
    scaled = (centered[:, None, None] * outer_rows.astype(jnp.float32)).astype(jnp.bfloat16)
    delta = jnp.einsum("imo,imc->oc", scaled, inner_cols, preferred_element_type=jnp.float32)
    members_all = fitness_all.shape[0]
    updated = (
        weight.astype(jnp.float32) + step_scale / math.sqrt(members_all * rank) * delta
    ).astype(jnp.bfloat16)
    return (output_full.reshape(tok_rows, out_cols).astype(jnp.bfloat16), updated)


def solution(mesh):
    in_specs = (
        P("pop", "tp"),
        P("pop", "tp"),
        P("pop", "tp"),
        P("pop", None, None),
        P("pop", None, "tp"),
    )
    out_specs = (P("pop", "tp"), P("pop", "tp"))
    return jax.shard_map(local, mesh=mesh, in_specs=in_specs, out_specs=out_specs, check_vma=False)
```

profile of v0, /device:TPU:1, one launch (start us, length us, event | category | flops | bytes accessed | tf_op | source)
XLA Modules:
  0.0 318.1 jit_solution(7085557132596609108)
XLA Ops:
  7.2 0.7 all-gather.4.cloned.1.call-update
  7.9 0.0 reduce-scatter.2.cloned.1.call-start
  8.0 97.6 %all-gather.4.cloned.1.call-done = bf16[5120,1280]{1,0:T(8,128)(2,1)} async-done(((bf16[80,1280]{1,0:T(8,128)(2,1)}), bf16[5120,1280]{1,0:T(8,128)(2,1)}) %all-gather.4.cloned.1.call-update) | async-done | bytes 13107216 | tf_op jit(solution)/shard_map/all_gather | solution.py:40
  105.5 20.6 %multiply_convert_fusion = bf16[1024,5120]{1,0:T(8,128)(2,1)} fusion(bf16[1024,1280]{1,0:T(8,128)(2,1)S(1)} %copy-done, bf16[5120,1280]{1,0:T(8,128)(2,1)} %all-gather.4.cloned.1.call-done), kind=kOutput, calls=%fused_computation | convolution fusion | flops 13432258560 | bytes 26214400 | tf_op jit(solution)/shard_map/dot_general | solution.py:38
  126.2 0.0 all-gather.6.cloned.1.call-start
  126.2 0.7 all-gather.6.cloned.1.call-update
  126.9 0.8 fusion.18
  127.7 0.7 broadcast_in_dim.2
  128.3 4.0 %all-to-all-start = ((f32[4,4,256,4]{2,3,1,0:T(4,128)}), f32[4,4,256,4]{2,3,1,0:T(4,128)S(1)}, u32[]{:S(2)}, u32[]{:S(2)}) async-start(f32[4,4,256,4]{2,3,1,0:T(4,128)} %broadcast_in_dim.2), calls=%async_computation.1 | async-start | bytes 131072 | tf_op jit(solution)/shard_map/all_to_all | solution.py:13
  132.3 5.2 %copy.12 = bf16[4,4,5120]{1,0,2:T(4,128)(2,1)} copy(bf16[4,4,5120]{2,1,0:T(4,128)(2,1)S(1)} %copy-done.2) | data formatting | bytes 327680 | tf_op args[3]
  137.5 11.2 %reshape.57 = bf16[64,2,640]{2,1,0:T(2,128)(2,1)} reshape(bf16[5120,4,4]{2,1,0:T(4,128)(2,1)} %bitcast.28) | data formatting | bytes 327680
  148.7 6.4 %all-to-all-start.1 = ((bf16[64,2,640]{2,1,0:T(2,128)(2,1)}), bf16[64,2,640]{2,1,0:T(2,128)(2,1)S(1)}, u32[]{:S(2)}, u32[]{:S(2)}) async-start(bf16[64,2,640]{2,1,0:T(2,128)(2,1)} %reshape.57), calls=%async_computation.2 | async-start | bytes 327680 | tf_op jit(solution)/shard_map/all_to_all | solution.py:58
  155.2 11.6 %all-to-all-done.1 = bf16[64,2,640]{2,1,0:T(2,128)(2,1)S(1)} async-done(((bf16[64,2,640]{2,1,0:T(2,128)(2,1)}), bf16[64,2,640]{2,1,0:T(2,128)(2,1)S(1)}, u32[]{:S(2)}, u32[]{:S(2)}) %all-to-all-start.1) | async-done | bytes 163872 | tf_op jit(solution)/shard_map/all_to_all | solution.py:58
  166.8 12.3 %reshape.58 = bf16[5120,4,4]{2,1,0:T(4,128)(2,1)} reshape(bf16[64,2,640]{2,1,0:T(2,128)(2,1)S(1)} %all-to-all-done.1) | data formatting | bytes 327680
  179.1 6.9 %copy.13 = f32[4,4,64,80]{3,0,2,1:T(4,128)S(1)} copy(bf16[4,4,64,80]{1,0,3,2:T(4,128)(2,1)} %bitcast.27) | data formatting | bytes 491520 | tf_op jit(solution)/shard_map/convert_element_type | solution.py:61
  186.0 37.5 %reduce-scatter.2.cloned.1.call-done = bf16[1024,1280]{1,0:T(8,128)(2,1)} async-done(((bf16[1024,5120]{1,0:T(8,128)(2,1)}), bf16[1024,1280]{1,0:T(8,128)(2,1)}) %reduce-scatter.2.cloned.1.call-update) | async-done | bytes 2621456 | tf_op jit(solution)/shard_map/reduce_scatter | solution.py:46
  223.4 7.2 %fusion = (f32[4]{0:T(128)S(1)}, bf16[4,256,1280]{2,1,0:T(8,128)(2,1)}) fusion(bf16[4,256,1280]{2,1,0:T(8,128)(2,1)} %bitcast.30, f32[4,256,4]{1,2,0:T(4,128)S(1)} %reduce_sum.36, bf16[4,4,5120]{2,1,0:T(4,128)(2,1)S(1)} %copy-done.2, s32[]{:T(128)S(6)} %select_n.3, bf16[4,256,1280]{2,1,0:T(8,128)(2,1)} %bitcast.31), kind=kOutput, calls=%fused_computation.2 | convolution fusion | flops 72089600 | bytes 7921684 | tf_op jit(solution)/shard_map/mkr,mrc->mkc/dot_general | solution.py:50
  230.6 0.1 multiply_dynamic-update-slice_fusion
  230.7 76.1 %all-reduce = f32[1024]{0:T(1024)S(1)} all-reduce(f32[1024]{0:T(1024)S(1)} %multiply_dynamic-update-slice_fusion), channel_id=2, replica_groups=mesh['pop'=64,'tp'=4] {'pop','tp'}, use_global_device_ids=true, to_apply=%add | all-reduce | flops 1024 | bytes 8192
  306.8 0.6 reduce_sum.39
  307.4 0.2 reshape.46
  307.6 0.1 reduce_sum.38
  308.3 0.1 sub.15
  308.5 3.1 fusion.12
  (15 shorter events, 0.1 us)
Async XLA Ops:
  7.2 98.4 %copy-start = (bf16[1024,1280]{1,0:T(8,128)(2,1)S(1)}, bf16[1024,1280]{1,0:T(8,128)(2,1)}, u32[]{:S(2)}) copy-start(bf16[1024,1280]{1,0:T(8,128)(2,1)} %param.5) | copy-start | bytes 7864324
  7.2 98.3 %all-gather.4.cloned.1.call-start = ((), (), s32[]{:S(2)}) async-start(), calls=%async_computation.3 | async-start | bytes 13312000 | tf_op jit(solution)/shard_map/all_gather | solution.py:40
  7.9 215.5 %reduce-scatter.2.cloned.1.call-start = ((), (), s32[]{:S(2)}) async-start(), calls=%async_computation.4 | async-start | bytes 13107200 | tf_op jit(solution)/shard_map/reduce_scatter | solution.py:46
  126.1 0.8 copy-start.3
  126.1 6.2 %copy-start.2 = (bf16[4,4,5120]{2,1,0:T(4,128)(2,1)S(1)}, bf16[4,4,5120]{2,1,0:T(4,128)(2,1)}, u32[]{:S(2)}) copy-start(bf16[4,4,5120]{2,1,0:T(4,128)(2,1)} %param.8) | copy-start | bytes 491524
  126.2 182.3 %all-gather.6.cloned.1.call-start = ((), (), s32[]{:S(2)}) async-start(), calls=%async_computation.5 | async-start | bytes 2662400 | tf_op jit(solution)/shard_map/all_gather | solution.py:59
  128.3 20.4 %all-to-all-start = ((f32[4,4,256,4]{2,3,1,0:T(4,128)}), f32[4,4,256,4]{2,3,1,0:T(4,128)S(1)}, u32[]{:S(2)}, u32[]{:S(2)}) async-start(f32[4,4,256,4]{2,3,1,0:T(4,128)} %broadcast_in_dim.2), calls=%async_computation.1 | async-start | bytes 131072 | tf_op jit(solution)/shard_map/all_to_all | solution.py:13
  148.7 18.1 %all-to-all-start.1 = ((bf16[64,2,640]{2,1,0:T(2,128)(2,1)}), bf16[64,2,640]{2,1,0:T(2,128)(2,1)S(1)}, u32[]{:S(2)}, u32[]{:S(2)}) async-start(bf16[64,2,640]{2,1,0:T(2,128)(2,1)} %reshape.57), calls=%async_computation.2 | async-start | bytes 327680 | tf_op jit(solution)/shard_map/all_to_all | solution.py:58
  186.0 122.5 %copy-start.1 = (bf16[80,1280]{1,0:T(8,128)(2,1)S(1)}, bf16[80,1280]{1,0:T(8,128)(2,1)}, u32[]{:S(2)}) copy-start(bf16[80,1280]{1,0:T(8,128)(2,1)} %param.7) | copy-start | bytes 614404
Sparse Core Ops, SparseCore 0:
  10.7 94.7 all-gather.3
  126.3 97.1 reduce-scatter.1
  226.2 77.3 all-gather.5
where the time goes:
time: 319 us; the launch traced here: 318 us
  waiting for transfers between devices  148 us (46%)
  blocking collectives  76.1 us (24%)
  local copies, waits for them, and re-layouts  36.6 us (11%)
  matrix products  31.7 us (10%)
  between operations  14.5 us (5%)
  starting transfers between devices  10.5 us (3%)
    all_gather x1, waiting for transfers between devices, local(): lax.all_gather(weight, 'pop', axis=0, tiled=True)  97.6 us
    unnamed x1, blocking collectives  76.1 us
    reduce_scatter x1, waiting for transfers between devices, local(): lax.psum_scatter(partial_terms.astype(jnp.bfloat16), 'tp', scatter_dimens...  37.5 us
    unnamed x12, local copies, waits for them, and re-layouts  28.7 us
    dot_general x1, matrix products, local(): lax.dot_general(tokens, lax.all_gather(weight, 'pop', axis=0, tiled=True)...  20.6 us
    all_to_all x1, waiting for transfers between devices, local(): lax.all_to_all(factor_out, 'pop', split_axis=2, concat_axis=0, tiled=True)  11.6 us
    dot_general x1, matrix products, local(): jnp.einsum('mkr,mrc->mkc', codes_sum, outer_cols, precision=lax.Precision...  7.16 us
    convert_element_type x1, local copies, waits for them, and re-layouts, local(): outer_rows.astype(jnp.float32)  6.9 us
  transfers between devices with their start and end apart: 5, of which 3 were waited for; matrix products, arithmetic and copies ran while one was open for 14% of the time, Pallas kernels for 0%

commit v1 on v0

--- a/solution.py
+++ b/solution.py
@@ -6,6 +6,16 @@
 
 noise_scale = 0.25
 step_scale = 10.0
+
+
+def _fill_packet(z, array_axis):
+    fresh = lax.all_to_all(
+        jnp.stack(lax.psum(1, axis_name="pop") * [z], axis=0),
+        split_axis=0,
+        axis_name="pop",
+        concat_axis=0,
+    )
+    return jnp.concatenate(fresh, axis=array_axis)
 
 
 def sent_to_all(shard, axis):
@@ -37,7 +47,7 @@
     partial_terms = (
         lax.dot_general(
             tokens,
-            lax.all_gather(weight, "pop", axis=0, tiled=True),
+            _fill_packet(weight, 0),
             (((1,), (1,)), ((), ())),
             preferred_element_type=jnp.float32,
         )

time: 319 us -> 528 us (1.66)
  blocking collectives: 76.1 us -> 376 us
  waiting for transfers between devices: 148 us -> 49.7 us
  local copies, waits for them, and re-layouts: 36.6 us -> 43.4 us
    all_to_all x0 -> x1, blocking collectives: none -> 301 us  [_fill_packet(): lax.all_to_all(jnp.stack(lax.psum(1, axis_name='pop') * [z], axis=0), spl...]
    all_gather x1 -> x0, waiting for transfers between devices: 97.6 us -> none  [local(): lax.all_gather(weight, 'pop', axis=0, tiled=True)]
    another operation x0 -> x1, local copies, waits for them, and re-layouts: none -> 6.64 us  [_fill_packet(): jnp.stack(lax.psum(1, axis_name='pop') * [z], axis=0)]
  transfers between devices with their start and end apart: 5 -> 4, of which waited for: 3 -> 2; matrix products, arithmetic and copies ran while one was open for 14% -> 9% of each run, Pallas kernels for 0% -> 0%
where the time goes in v1:
time: 528 us
  blocking collectives  376 us (71%)
  waiting for transfers between devices  49.7 us (9%)
  local copies, waits for them, and re-layouts  43.4 us (8%)
  matrix products  31.7 us (6%)
  between operations  16.2 us (3%)
  starting transfers between devices  9.97 us (2%)
    all_to_all x1, blocking collectives, _fill_packet(): lax.all_to_all(jnp.stack(lax.psum(1, axis_name='pop') * [z], axis=0), spl...  301 us
    unnamed x1, blocking collectives  75.4 us
    reduce_scatter x1, waiting for transfers between devices, local(): lax.psum_scatter(partial_terms.astype(jnp.bfloat16), 'tp', scatter_dimens...  37.3 us
    unnamed x12, local copies, waits for them, and re-layouts  28.9 us
    dot_general x1, matrix products, local(): lax.dot_general(tokens, _fill_packet(weight, 0), (((1,), (1,)), ((), ()))...  20.6 us
    all_to_all x1, waiting for transfers between devices, local(): lax.all_to_all(factor_out, 'pop', split_axis=2, concat_axis=0, tiled=True)  11.8 us
  transfers between devices with their start and end apart: 4, of which 2 were waited for; matrix products, arithmetic and copies ran while one was open for 9% of the time, Pallas kernels for 0%

profile of v1, /device:TPU:1, one launch (start us, length us, event | category | flops | bytes accessed | tf_op | source)
XLA Modules:
  0.0 527.8 jit_solution(7769528666398566438)
XLA Ops:
  8.1 6.6 %stack.2 = bf16[64,80,1280]{2,1,0:T(8,128)(2,1)} broadcast(bf16[80,1280]{1,0:T(8,128)(2,1)} %param.7), dimensions={1,2} | broadcast | bytes 13312000 | tf_op jit(solution)/shard_map/stack | solution.py:13
  14.7 300.7 %all_to_all.19 = bf16[64,80,1280]{2,1,0:T(8,128)(2,1)} all-to-all(bf16[64,80,1280]{2,1,0:T(8,128)(2,1)} %stack.2), channel_id=1, replica_groups=mesh['pop'=64,'tp'=4] {'pop'}, dimensions={0} | all-to-all | bytes 26214400 | tf_op jit(solution)/shard_map/all_to_all | solution.py:12
  315.4 20.6 %multiply_convert_fusion = bf16[1024,5120]{1,0:T(8,128)(2,1)} fusion(bf16[1024,1280]{1,0:T(8,128)(2,1)S(1)} %copy-done, bf16[5120,1280]{1,0:T(8,128)(2,1)} %bitcast.30), kind=kOutput, calls=%fused_computation | convolution fusion | flops 13432258560 | bytes 26214400 | tf_op jit(solution)/shard_map/dot_general | solution.py:48
  336.0 0.0 all-gather.3.cloned.1.call-start
  336.1 0.5 all-gather.3.cloned.1.call-update
  336.6 0.2 copy-done.3
  336.8 0.8 fusion.18
  337.5 0.7 broadcast_in_dim.2
  338.2 4.0 all-to-all-start.1
  342.2 5.2 copy.12
  347.4 11.2 %reshape.63 = bf16[64,2,640]{2,1,0:T(2,128)(2,1)} reshape(bf16[5120,4,4]{2,1,0:T(4,128)(2,1)} %bitcast.29) | data formatting | bytes 327680
  358.7 5.9 %all-to-all-start.2 = ((bf16[64,2,640]{2,1,0:T(2,128)(2,1)}), bf16[64,2,640]{2,1,0:T(2,128)(2,1)S(1)}, u32[]{:S(2)}, u32[]{:S(2)}) async-start(bf16[64,2,640]{2,1,0:T(2,128)(2,1)} %reshape.63), calls=%async_computation.3 | async-start | bytes 327680 | tf_op jit(solution)/shard_map/all_to_all | solution.py:68
  364.6 11.8 %all-to-all-done.2 = bf16[64,2,640]{2,1,0:T(2,128)(2,1)S(1)} async-done(((bf16[64,2,640]{2,1,0:T(2,128)(2,1)}), bf16[64,2,640]{2,1,0:T(2,128)(2,1)S(1)}, u32[]{:S(2)}, u32[]{:S(2)}) %all-to-all-start.2) | async-done | bytes 163872 | tf_op jit(solution)/shard_map/all_to_all | solution.py:68
  376.4 12.3 %reshape.64 = bf16[5120,4,4]{2,1,0:T(4,128)(2,1)} reshape(bf16[64,2,640]{2,1,0:T(2,128)(2,1)S(1)} %all-to-all-done.2) | data formatting | bytes 327680
  388.7 6.9 %copy.13 = f32[4,4,64,80]{3,0,2,1:T(4,128)S(1)} copy(bf16[4,4,64,80]{1,0,3,2:T(4,128)(2,1)} %bitcast.28) | data formatting | bytes 491520 | tf_op jit(solution)/shard_map/convert_element_type | solution.py:71
  395.6 37.3 %reduce-scatter.2.cloned.1.call-done = bf16[1024,1280]{1,0:T(8,128)(2,1)} async-done(((bf16[1024,5120]{1,0:T(8,128)(2,1)}), bf16[1024,1280]{1,0:T(8,128)(2,1)}) %reduce-scatter.2.cloned.1.call-update) | async-done | bytes 2621456 | tf_op jit(solution)/shard_map/reduce_scatter | solution.py:56
  432.9 7.2 %fusion = (f32[4]{0:T(128)S(1)}, bf16[4,256,1280]{2,1,0:T(8,128)(2,1)}) fusion(bf16[4,256,1280]{2,1,0:T(8,128)(2,1)} %bitcast.32, f32[4,256,4]{1,2,0:T(4,128)S(1)} %reduce_sum.36, bf16[4,4,5120]{2,1,0:T(4,128)(2,1)S(1)} %copy-done.2, s32[]{:T(128)S(6)} %select_n.3, bf16[4,256,1280]{2,1,0:T(8,128)(2,1)} %bitcast.33), kind=kOutput, calls=%fused_computation.2 | convolution fusion | flops 72089600 | bytes 7921684 | tf_op jit(solution)/shard_map/mkr,mrc->mkc/dot_general | solution.py:60
  440.0 0.1 multiply_dynamic-update-slice_fusion
  440.1 75.4 %all-reduce = f32[1024]{0:T(1024)S(1)} all-reduce(f32[1024]{0:T(1024)S(1)} %multiply_dynamic-update-slice_fusion), channel_id=2, replica_groups=mesh['pop'=64,'tp'=4] {'pop','tp'}, use_global_device_ids=true, to_apply=%add | all-reduce | flops 1024 | bytes 8192
  515.5 0.2 reshape.52
  515.7 0.6 reduce_sum.39
  516.3 0.1 reduce_sum.38
  517.1 0.1 sub.15
  517.2 3.1 fusion.12
  (14 shorter events, 0.1 us)
Async XLA Ops:
  8.0 307.4 %copy-start = (bf16[1024,1280]{1,0:T(8,128)(2,1)S(1)}, bf16[1024,1280]{1,0:T(8,128)(2,1)}, u32[]{:S(2)}) copy-start(bf16[1024,1280]{1,0:T(8,128)(2,1)} %param.5) | copy-start | bytes 7864324
  8.0 424.9 %reduce-scatter.2.cloned.1.call-start = ((), (), s32[]{:S(2)}) async-start(), calls=%async_computation.4 | async-start | bytes 13107200 | tf_op jit(solution)/shard_map/reduce_scatter | solution.py:56
  336.0 0.8 copy-start.3
  336.0 6.2 %copy-start.2 = (bf16[4,4,5120]{2,1,0:T(4,128)(2,1)S(1)}, bf16[4,4,5120]{2,1,0:T(4,128)(2,1)}, u32[]{:S(2)}) copy-start(bf16[4,4,5120]{2,1,0:T(4,128)(2,1)} %param.8) | copy-start | bytes 491524
  336.0 181.2 %all-gather.3.cloned.1.call-start = ((), (), s32[]{:S(2)}) async-start(), calls=%async_computation.5 | async-start | bytes 2662400 | tf_op jit(solution)/shard_map/all_gather | solution.py:69
  338.2 20.4 %all-to-all-start.1 = ((f32[4,4,256,4]{2,3,1,0:T(4,128)}), f32[4,4,256,4]{2,3,1,0:T(4,128)S(1)}, u32[]{:S(2)}, u32[]{:S(2)}) async-start(f32[4,4,256,4]{2,3,1,0:T(4,128)} %broadcast_in_dim.2), calls=%async_computation.2 | async-start | bytes 131072 | tf_op jit(solution)/shard_map/all_to_all | solution.py:23
  358.7 17.7 %all-to-all-start.2 = ((bf16[64,2,640]{2,1,0:T(2,128)(2,1)}), bf16[64,2,640]{2,1,0:T(2,128)(2,1)S(1)}, u32[]{:S(2)}, u32[]{:S(2)}) async-start(bf16[64,2,640]{2,1,0:T(2,128)(2,1)} %reshape.63), calls=%async_computation.3 | async-start | bytes 327680 | tf_op jit(solution)/shard_map/all_to_all | solution.py:68
  395.6 121.7 %copy-start.1 = (bf16[80,1280]{1,0:T(8,128)(2,1)S(1)}, bf16[80,1280]{1,0:T(8,128)(2,1)}, u32[]{:S(2)}) copy-start(bf16[80,1280]{1,0:T(8,128)(2,1)} %param.7) | copy-start | bytes 614404
Sparse Core Ops, SparseCore 0:
  336.1 96.6 reduce-scatter.1
Sparse Core Ops, SparseCore 1:
  339.2 74.4 all-gather.2
